TPU v7x, 32 devices: a whole 2x2x4 slice. The times are simulated.
32 devices in a mesh: pair: 4 (over y, x), virt: 8 (over z, core).
Axes of the slice: x: 2, y: 2, z: 4, core: 2. Of those that a mesh axis runs over, the one named last changes fastest.
Arguments:
- density_row_blocks: bfloat16 [160, 128, 2744], P('pair', 'virt'), may hold values from -6 to 6
- vir_left: bfloat16 [128, 2744], P('virt'), may hold values from -0.046875 to 0.046875
- vir_right: bfloat16 [128, 2744], P('virt'), may hold values from -0.109375 to 0.109375
- orb_energy: bfloat16 [128], P('virt'), may hold values from 0.5 to 3
- state_energy: float32 [8], replicated, may hold values from -1 to -0.1
- bra_ket_states: int32 [160, 2], P('pair'), may hold values from 0 to 7
- row_block_starts: int32 [160], P('pair'), may hold values from 0 to 2616
Outputs:
- slot_couplings: float32 [160], P('pair')
- heff: float32 [8, 8], replicated
All inputs are finite; a program needn't handle non-finite values.
Results may differ from a plain program's by a relative error of at most 0.0003.
Values may be sent and summed in bfloat16 or wider, within the bound.
A program may use at most 64 MiB of HBM per device.

v0:
```python
import jax
import jax.numpy as jnp
from jax import lax
from jax.sharding import PartitionSpec as P


def local(
    density_row_blocks,
    vir_left,
    vir_right,
    orb_energy,
    state_energy,
    bra_ket_states,
    row_block_starts,
):
    slots, rows, ntrip = density_row_blocks.shape
    nstate = state_energy.shape[0]
    virt_index = lax.axis_index("virt")
    positions = (
        row_block_starts[:, None] + virt_index * rows + jnp.arange(rows, dtype=jnp.int32)[None, :]
    )
    positions = positions.reshape(slots * rows)
    flat_rdm = density_row_blocks.reshape(slots * rows, ntrip)
    states = jnp.arange(nstate, dtype=jnp.int32)
    first = (bra_ket_states[:, 0:1] == states[None, :]).astype(jnp.float32)
    second = (bra_ket_states[:, 1:2] == states[None, :]).astype(jnp.float32)
    shift = jnp.dot(first + second, state_energy, precision=lax.Precision.HIGHEST)
    columns = jnp.take(lax.all_gather(vir_left, "virt", axis=0, tiled=True), positions, axis=1)
    right_piece = lax.all_gather(vir_right, "virt", axis=0, tiled=True)
    count = right_piece.shape[0]
    contracted = lax.dot_general(
        right_piece, flat_rdm, (((1,), (1,)), ((), ())), preferred_element_type=jnp.float32
    )
    inverse = 1.0 / (
        lax.all_gather(orb_energy, "virt", axis=0, tiled=True).astype(jnp.float32)[:, None]
        - shift[None, :]
    )
    product = columns.astype(jnp.float32).reshape(count, slots, rows) * contracted.reshape(
        count, slots, rows
    )
    partial_sums = jnp.sum(jnp.sum(product, axis=2) * inverse, axis=0)
    couplings = lax.psum(partial_sums, "virt")
    local_sum = jnp.dot(first.T, couplings[:, None] * second, precision=lax.Precision.HIGHEST)
    collected = lax.all_gather(local_sum[None], "pair", axis=0, tiled=True)
    coupling_sum = jnp.sum(collected, axis=0)
    heff = jnp.diag(state_energy) + 0.5 * (coupling_sum + coupling_sum.T)
    return (couplings, heff)


def solution(mesh):
    placed = (
        P("pair", "virt", None),
        P("virt", None),
        P("virt", None),
        P("virt"),
        P(),
        P("pair", None),
        P("pair"),
    )
    return jax.shard_map(
        local, mesh=mesh, in_specs=placed, out_specs=(P("pair"), P()), check_vma=False
    )
```

profile of v0, /device:TPU:0, one launch (start us, length us, event | category | flops | bytes accessed | tf_op | source)
XLA Modules:
  0.0 82.9 jit_solution(17060475857912333870)
XLA Ops:
  0.6 0.0 copy-start
  0.6 0.7 broadcast_add_fusion
  1.3 0.1 copy.22
  1.4 0.1 add.74
  1.5 17.2 %all_gather.12 = bf16[128,2744]{1,0:T(8,128)(2,1)S(1)} all-gather(bf16[16,2744]{1,0:T(8,128)(2,1)} %param.8), channel_id=1, replica_groups=mesh['pair'=4,'virt'=8] {'virt'}, dimensions={0}, use_global_device_ids=true | all-gather | bytes 790272 | tf_op jit(solution)/shard_map/all_gather | solution.py:28
  18.8 0.4 copy.23
  19.1 2.0 %gather_fusion = bf16[640,128]{1,0:T(8,128)(2,1)S(1)} fusion(bf16[128,2744]{0,1:T(8,128)(2,1)S(1)} %copy.23, s32[1024]{0:T(1024)S(1)} %pad_clamp_fusion), kind=kCustom, calls=%fused_computation | custom fusion | bytes 330240 | tf_op jit(solution)/shard_map/jit(_take)/gather | solution.py:28
  21.1 0.0 copy-start.1
  21.2 0.0 copy-start.2
  21.2 0.0 copy-start.4
  21.2 0.0 copy-start.3
  21.2 0.0 copy-done
  21.2 15.5 %all_gather.13 = bf16[128,2744]{1,0:T(8,128)(2,1)S(1)} all-gather(bf16[16,2744]{1,0:T(8,128)(2,1)S(1)} %copy-done), channel_id=1, replica_groups=mesh['pair'=4,'virt'=8] {'virt'}, dimensions={0}, use_global_device_ids=true | all-gather | bytes 790272 | tf_op jit(solution)/shard_map/all_gather | solution.py:29
  36.7 3.8 %fusion.5 = f32[128,40]{0,1:T(8,128)S(1)} fusion(bf16[40,16,2744]{2,1,0:T(8,128)(2,1)} %param.7, bf16[128,2744]{1,0:T(8,128)(2,1)S(1)} %all_gather.13, bf16[128,40,16]{0,2,1:T(8,128)(2,1)S(1)} %bitcast.24, pred[40,16]{0,1:T(8,128)(4,1)S(1)} %compare_and_fusion), kind=kOutput, calls=%fused_computation.4 | convolution fusion | flops 449899520 | bytes 4399744 | tf_op jit(solution)/shard_map/dot_general | solution.py:31
  40.5 0.0 copy-done.1
  40.5 0.0 copy-done.2
  40.5 0.2 convolution_bitcast_fusion
  40.7 0.0 copy-done.4
  40.7 0.6 dynamic-slice
  42.0 0.0 copy-done.3
  42.0 0.2 dynamic-update-slice
  42.2 17.7 %all-reduce = bf16[128]{0:T(256)(128)(2,1)S(1)} all-reduce(bf16[128]{0:T(256)(128)(2,1)S(1)} %dynamic-update-slice), channel_id=1, replica_groups=mesh['pair'=4,'virt'=8] {'virt'}, use_global_device_ids=true, to_apply=%add | all-reduce | flops 128 | bytes 512
  60.0 0.2 multiply_reduce_fusion
  60.1 13.6 %psum.7 = f32[40]{0:T(128)S(1)} all-reduce(f32[40]{0:T(128)S(1)} %multiply_reduce_fusion), channel_id=1, replica_groups=mesh['pair'=4,'virt'=8] {'virt'}, use_global_device_ids=true, to_apply=%region_2.3 | all-reduce | flops 40 | bytes 320 | tf_op jit(solution)/shard_map/psum | solution.py:42
  73.7 0.0 copy-start.5
  73.7 0.3 fusion.9
  74.0 8.2 %all-gather = f32[32,8]{1,0:T(8,128)S(1)} all-gather(f32[8,8]{1,0:T(8,128)S(1)} %fusion.9), channel_id=2, replica_groups=mesh['pair'=4,'virt'=8] {'pair'}, dimensions={0}, use_global_device_ids=true | all-gather | bytes 1280 | tf_op jit(solution)/shard_map/all_gather | solution.py:44
  82.2 0.1 copy.26
  82.3 0.7 fusion.21
  82.9 0.0 copy-done.5
  (8 shorter events, 0.1 us)
Async XLA Ops:
  0.6 20.6 %copy-start = (bf16[16,2744]{1,0:T(8,128)(2,1)S(1)}, bf16[16,2744]{1,0:T(8,128)(2,1)}, u32[]{:S(2)}) copy-start(bf16[16,2744]{1,0:T(8,128)(2,1)} %param.9) | copy-start | bytes 263428
  21.1 19.3 %copy-start.1 = (s32[40,2]{0,1:T(2,128)S(1)}, s32[40,2]{0,1:T(2,128)}, u32[]{:S(2)}) copy-start(s32[40,2]{0,1:T(2,128)} %param.12) | copy-start | bytes 964
  21.2 19.3 %copy-start.2 = (f32[8]{0:T(128)S(1)}, f32[8]{0:T(128)}, u32[]{:S(2)}) copy-start(f32[8]{0:T(128)} %param.11) | copy-start | bytes 100
  21.2 19.5 %copy-start.4 = (u32[32]{0:T(128)S(1)}, u32[32]{0:T(128)}, u32[]{:S(2)}) copy-start(u32[32]{0:T(128)} %constant.33) | copy-start | bytes 388
  21.2 20.8 %copy-start.3 = (bf16[16]{0:T(256)(128)(2,1)S(1)}, bf16[16]{0:T(256)(128)(2,1)}, u32[]{:S(2)}) copy-start(bf16[16]{0:T(256)(128)(2,1)} %param.10) | copy-start | bytes 100
  73.7 9.2 %copy-start.5 = (f32[40]{0:T(128)}, f32[40]{0:T(128)S(1)}, u32[]{:S(2)}) copy-start(f32[40]{0:T(128)S(1)} %psum.7) | copy-start | bytes 484
where the time goes:
time: 83.2 us; the launch traced here: 82.9 us
  blocking collectives  72.2 us (87%)
  matrix products  4.26 us (5%)
  local copies, waits for them, and re-layouts  3.48 us (4%)
  other arithmetic  1.59 us (2%)
  between operations  1.41 us (2%)
    unnamed x1, blocking collectives  17.7 us
    all_gather x1, blocking collectives, local(): lax.all_gather(vir_left, 'virt', axis=0, tiled=True)  17.2 us
    all_gather x1, blocking collectives, local(): right_piece = lax.all_gather(vir_right, 'virt', axis=0, tiled=True)  15.5 us
    psum x1, blocking collectives, local(): couplings = lax.psum(partial_sums, 'virt')  13.6 us
    all_gather x1, blocking collectives, local(): collected = lax.all_gather(local_sum[None], 'pair', axis=0, tiled=True)  8.18 us
    dot_general x1, matrix products, local(): lax.dot_general(right_piece, flat_rdm, (((1,), (1,)), ((), ())), preferre...  3.8 us
    gather x1, local copies, waits for them, and re-layouts, local(): jnp.take(lax.all_gather(vir_left, 'virt', axis=0, tiled=True), positions,...  1.99 us

commit v1 on v0

v1 whole, which is shorter than its diff:
```python
import functools

import jax
import jax.numpy as jnp
from jax import lax
from jax.experimental import pallas as pl
from jax.experimental.pallas import tpu as pltpu
from jax.sharding import PartitionSpec as P

MESH = pl.DeviceIdType.MESH
LANES = 128


def windows(
    l_raw,
    e_ref,
    se_ref,
    states_ref,
    starts_ref,
    w_send,
    shift_ref,
    bra_ref,
    ket_ref,
    l_f32,
):
    nvirt, avirt, _ = w_send.shape
    ntrip = l_raw.shape[1]
    slots = starts_ref.shape[0]
    rows = shift_ref.shape[1] // slots
    group = LANES // rows
    blocks = slots // group

    l_f32[...] = jnp.zeros_like(l_f32)
    l_f32[:, :ntrip] = l_raw[...].astype(jnp.float32)
    lane = lax.broadcasted_iota(jnp.int32, (avirt, LANES), 1) // rows
    width = rows * nvirt
    load_width = width + LANES

    def window_block(b, carry):
        views = []
        for j in range(group):
            offset = starts_ref[b * group + j]
            rest = offset % LANES
            base = pl.multiple_of(offset - rest, LANES)
            wide = l_f32[:, pl.ds(base, load_width)]
            turned = pltpu.roll(wide, (load_width - rest) % load_width, 1)
            views.append(turned[:, :width])
        for q in range(nvirt // group):
            held = [v[:, q * LANES : (q + 1) * LANES] for v in views]
            bit = 1
            while bit < group:
                keep = (lane & bit) == 0
                fresh = list(held)
                for j in range(group):
                    if j & bit == 0:
                        a, o = held[j], held[j | bit]
                        fresh[j] = jnp.where(keep, a, pltpu.roll(o, bit * rows, 1))
                        fresh[j | bit] = jnp.where(keep, pltpu.roll(a, LANES - bit * rows, 1), o)
                held = fresh
                bit *= 2
            for i in range(group):
                w_send[q * group + i, :, pl.ds(pl.multiple_of(b * LANES, LANES), LANES)] = held[
                    i
                ].astype(jnp.bfloat16)
        return carry

    lax.fori_loop(0, blocks, window_block, 0)
    square = (
        lax.broadcasted_iota(jnp.int32, (avirt, avirt), 0)
        == lax.broadcasted_iota(jnp.int32, (avirt, avirt), 1)
    )
    energy_own = jnp.sum(
        jnp.where(square, e_ref[...].astype(jnp.float32), 0.0), axis=1, keepdims=True
    )
    energy_own = jnp.broadcast_to(energy_own, (avirt, LANES)).astype(jnp.bfloat16)
    for i in range(nvirt):
        w_send[i, :, blocks * LANES :] = energy_own

    wide_lane = lax.broadcasted_iota(jnp.int32, (1, LANES), 1)
    bra = jnp.full((1, LANES), -1, jnp.int32)
    ket = jnp.full((1, LANES), -1, jnp.int32)
    shifts = []
    for b in range(blocks):
        shift = jnp.zeros((1, LANES), jnp.float32)
        for j in range(group):
            s = b * group + j
            i_state, j_state = states_ref[s], states_ref[slots + s]
            total = se_ref[i_state] + se_ref[j_state]
            shift = jnp.where(wide_lane // rows == j, total, shift)
            bra = jnp.where(wide_lane == s, i_state, bra)
            ket = jnp.where(wide_lane == s, j_state, ket)
        shifts.append(shift)
    shift_ref[...] = jnp.concatenate(shifts, axis=1)
    bra_ref[...] = bra
    ket_ref[...] = ket


def kernel(
    npair,
    nvirt,
    chunks,
    d_hbm,
    r_hbm,
    w_send,
    shift_ref,
    bra_ref,
    ket_ref,
    se_ref,
    coup_ref,
    heff_ref,
    d_all,
    r_all,
    w_all,
    p_send,
    p_all,
    h_send,
    h_all,
    d_sem,
    o_sem,
    own_sem,
    r_ssem,
    r_rsem,
    f_ssem,
    w_ssem,
    w_rsem,
    p_ssem,
    p_rsem,
    h_ssem,
    h_rsem,
):
    slots, rows, ntrip = d_all.shape
    nstate = heff_ref.shape[0]
    avirt = r_all.shape[1]
    nz = nvirt // 2
    group = LANES // rows
    blocks = slots // group
    me = lax.axis_index("virt")
    my_pair = lax.axis_index("pair")
    my_z, my_c = me // 2, me % 2
    sibling = my_z * 2 + 1 - my_c
    z_order = sorted(range(1, nz), key=lambda d: -min(d, nz - d))

    r_copy = pltpu.make_async_copy(r_hbm, r_all.at[me], o_sem)
    r_copy.start()
    d_copy = pltpu.make_async_copy(d_hbm, d_all, d_sem)
    d_copy.start()

    barrier = pltpu.get_barrier_semaphore()
    for k in range(1, nvirt):
        pl.semaphore_signal(
            barrier, inc=1, device_id={"virt": (me + k) % nvirt}, device_id_type=MESH
        )
    for k in range(1, npair):
        pl.semaphore_signal(
            barrier, inc=1, device_id={"pair": (my_pair + k) % npair}, device_id_type=MESH
        )
    pl.semaphore_wait(barrier, nvirt + npair - 2)

    r_copy.wait()

    def piece(source, c):
        lo, width = chunks[c]
        return r_all.at[source, :, pl.ds(lo, width)]

    def send_right(source, c, target, send_sem):
        return pltpu.make_async_remote_copy(
            src_ref=piece(source, c),
            dst_ref=piece(source, c),
            send_sem=send_sem,
            recv_sem=r_rsem.at[source, c],
            device_id={"virt": target},
            device_id_type=MESH,
        )

    sends = []
    for c in range(len(chunks)):
        for n, dz in enumerate(z_order):
            target = ((my_z + dz) % nz) * 2 + my_c
            sends.append(send_right(me, c, target, r_ssem.at[n, c]))
            sends[-1].start()
        sends.append(send_right(me, c, sibling, r_ssem.at[nz - 1, c]))
        sends[-1].start()

    def send_window(k):
        target = (me + k) % nvirt
        return pltpu.make_async_remote_copy(
            src_ref=w_send.at[target],
            dst_ref=w_all.at[me],
            send_sem=w_ssem.at[k],
            recv_sem=w_rsem.at[me],
            device_id={"virt": target},
            device_id_type=MESH,
        )

    for k in range(1, nvirt):
        sends.append(send_window(k))
        sends[-1].start()
    own = pltpu.make_async_copy(w_send.at[me], w_all.at[me], own_sem)
    own.start()

    for c in range(len(chunks)):
        for dz in range(1, nz):
            source = ((my_z + dz) % nz) * 2 + my_c
            send_right(source, c, sibling, f_ssem.at[dz, c]).wait_recv()
            forward = send_right(source, c, sibling, f_ssem.at[dz, c])
            forward.start()
            sends.append(forward)
    d_copy.wait()
    total = None
    for c, (lo, cw) in enumerate(chunks):
        for dz in range(nz):
            source = ((my_z + dz) % nz) * 2 + 1 - my_c
            send_right(source, c, sibling, f_ssem.at[0, c]).wait_recv()
        part = lax.dot_general(
            r_all[:, :, lo : lo + cw].reshape(nvirt * avirt, cw),
            d_all[:, :, lo : lo + cw].reshape(slots * rows, cw),
            (((1,), (1,)), ((), ())),
            preferred_element_type=jnp.float32,
        )
        total = part if total is None else total + part
    own.wait()
    for k in range(1, nvirt):
        source = (me + k) % nvirt
        pltpu.make_async_remote_copy(
            src_ref=w_send.at[source],
            dst_ref=w_all.at[source],
            send_sem=w_ssem.at[0],
            recv_sem=w_rsem.at[source],
            device_id={"virt": source},
            device_id_type=MESH,
        ).wait_recv()
    columns = w_all[:, :, : blocks * LANES].reshape(nvirt * avirt, blocks * LANES)
    energy = w_all[:, :, blocks * LANES :].reshape(nvirt * avirt, LANES)[:, :1]
    inverse = 1.0 / (energy.astype(jnp.float32) - shift_ref[...])
    summed = jnp.sum(total * columns.astype(jnp.float32) * inverse, axis=0, keepdims=True)
    gather_lanes = (
        lax.broadcasted_iota(jnp.int32, (slots * rows, LANES), 0) // rows
        == lax.broadcasted_iota(jnp.int32, (slots * rows, LANES), 1)
    ).astype(jnp.float32)
    partial = jnp.dot(
        jnp.broadcast_to(summed, (8, slots * rows)),
        gather_lanes,
        precision=lax.Precision.HIGHEST,
        preferred_element_type=jnp.float32,
    )[:1]

    p_send[...] = partial
    for k in range(1, nvirt):
        target = (me + k) % nvirt
        sends.append(
            pltpu.make_async_remote_copy(
                src_ref=p_send,
                dst_ref=p_all.at[me],
                send_sem=p_ssem.at[k],
                recv_sem=p_rsem.at[me],
                device_id={"virt": target},
                device_id_type=MESH,
            )
        )
        sends[-1].start()
    p_all[me] = partial
    for k in range(1, nvirt):
        source = (me + k) % nvirt
        pltpu.make_async_remote_copy(
            src_ref=p_send,
            dst_ref=p_all.at[source],
            send_sem=p_ssem.at[0],
            recv_sem=p_rsem.at[source],
            device_id={"virt": source},
            device_id_type=MESH,
        ).wait_recv()
    couplings = jnp.sum(p_all[...], axis=0)
    coup_ref[...] = couplings[:, :slots]

    row = lax.broadcasted_iota(jnp.int32, (nstate, LANES), 0)
    first = (row == bra_ref[...]).astype(jnp.float32)
    second = (row == ket_ref[...]).astype(jnp.float32)
    over_lanes = (((1,), (1,)), ((), ()))
    direct = lax.dot_general(
        first * couplings, second, over_lanes, precision=lax.Precision.HIGHEST,
        preferred_element_type=jnp.float32,
    )
    turned = lax.dot_general(
        second * couplings, first, over_lanes, precision=lax.Precision.HIGHEST,
        preferred_element_type=jnp.float32,
    )
    both = direct + turned
    h_send[...] = jnp.concatenate(
        [both, jnp.zeros((nstate, LANES - nstate), jnp.float32)], axis=1
    )
    for k in range(1, npair):
        target = (my_pair + k) % npair
        sends.append(
            pltpu.make_async_remote_copy(
                src_ref=h_send,
                dst_ref=h_all.at[my_pair],
                send_sem=h_ssem.at[k],
                recv_sem=h_rsem.at[my_pair],
                device_id={"pair": target},
                device_id_type=MESH,
            )
        )
        sends[-1].start()
    h_all[my_pair] = h_send[...]
    si = lax.broadcasted_iota(jnp.int32, (nstate, nstate), 0)
    sj = lax.broadcasted_iota(jnp.int32, (nstate, nstate), 1)
    diagonal = jnp.zeros((nstate, nstate), jnp.float32)
    for n in range(nstate):
        diagonal = jnp.where((si == n) & (sj == n), se_ref[n], diagonal)
    for k in range(1, npair):
        source = (my_pair + k) % npair
        pltpu.make_async_remote_copy(
            src_ref=h_send,
            dst_ref=h_all.at[source],
            send_sem=h_ssem.at[0],
            recv_sem=h_rsem.at[source],
            device_id={"pair": source},
            device_id_type=MESH,
        ).wait_recv()
    heff_ref[...] = diagonal + 0.5 * jnp.sum(h_all[...], axis=0)[:, :nstate]
    for send in sends:
        send.wait_send()


def local(
    npair,
    nvirt,
    density_row_blocks,
    vir_left,
    vir_right,
    orb_energy,
    state_energy,
    bra_ket_states,
    row_block_starts,
):
    slots, rows, ntrip = density_row_blocks.shape
    avirt = vir_left.shape[0]
    nstate = state_energy.shape[0]
    padded = -(-ntrip // LANES) * LANES
    half = -(-(padded // LANES) // 2) * LANES
    chunks = ((0, half), (half, ntrip - half))
    nch = len(chunks)
    wide = slots * rows + LANES
    any_space = pl.BlockSpec(memory_space=pltpu.HBM)
    vmem = pl.BlockSpec(memory_space=pltpu.VMEM)
    smem = pl.BlockSpec(memory_space=pltpu.SMEM)
    dma = pltpu.SemaphoreType.DMA
    w_send, shift, bra, ket = pl.pallas_call(
        windows,
        out_shape=(
            jax.ShapeDtypeStruct((nvirt, avirt, wide), jnp.bfloat16),
            jax.ShapeDtypeStruct((1, slots * rows), jnp.float32),
            jax.ShapeDtypeStruct((1, LANES), jnp.int32),
            jax.ShapeDtypeStruct((1, LANES), jnp.int32),
        ),
        in_specs=[vmem, vmem, smem, smem, smem],
        out_specs=(vmem,) * 4,
        scratch_shapes=[pltpu.VMEM((avirt, padded + nvirt * rows), jnp.float32)],
    )(
        vir_left,
        orb_energy.reshape(1, avirt),
        state_energy,
        bra_ket_states.T.reshape(2 * slots),
        row_block_starts,
    )
    couplings, heff = pl.pallas_call(
        functools.partial(kernel, npair, nvirt, chunks),
        out_shape=(
            jax.ShapeDtypeStruct((1, slots), jnp.float32),
            jax.ShapeDtypeStruct((nstate, nstate), jnp.float32),
        ),
        in_specs=[any_space, any_space, vmem, vmem, vmem, vmem, smem],
        out_specs=(vmem, vmem),
        scratch_shapes=[
            pltpu.VMEM((slots, rows, ntrip), jnp.bfloat16),
            pltpu.VMEM((nvirt, avirt, ntrip), jnp.bfloat16),
            pltpu.VMEM((nvirt, avirt, wide), jnp.bfloat16),
            pltpu.VMEM((1, LANES), jnp.float32),
            pltpu.VMEM((nvirt, 1, LANES), jnp.float32),
            pltpu.VMEM((nstate, LANES), jnp.float32),
            pltpu.VMEM((npair, nstate, LANES), jnp.float32),
            dma,
            dma,
            dma,
            dma((nvirt // 2, nch)),
            dma((nvirt, nch)),
            dma((nvirt // 2, nch)),
            dma((nvirt,)),
            dma((nvirt,)),
            dma((nvirt,)),
            dma((nvirt,)),
            dma((npair,)),
            dma((npair,)),
        ],
        compiler_params=pltpu.CompilerParams(
            collective_id=0, has_side_effects=True, vmem_limit_bytes=60 * 1024 * 1024
        ),
    )(
        density_row_blocks,
        vir_right,
        w_send,
        shift,
        bra,
        ket,
        state_energy,
    )
    return couplings.reshape(slots), heff


def solution(mesh):
    npair, nvirt = mesh.shape["pair"], mesh.shape["virt"]
    placed = (
        P("pair", "virt", None),
        P("virt", None),
        P("virt", None),
        P("virt"),
        P(),
        P("pair", None),
        P("pair"),
    )
    return jax.shard_map(
        functools.partial(local, npair, nvirt),
        mesh=mesh,
        in_specs=placed,
        out_specs=(P("pair"), P()),
        check_vma=False,
    )
```

time: 83.2 us -> 37 us (0.44)
  blocking collectives: 72.2 us -> 0 us
  Pallas kernels: 0 us -> 32.5 us
  matrix products: 4.26 us -> 0 us
  other arithmetic: 1.59 us -> 0 us
    all_gather x3 -> x0, blocking collectives: 40.9 us -> none  [the longest x1 17.2 us: local(): lax.all_gather(vir_left, 'virt', axis=0, tiled=True)]
    pallas_call x0 -> x2, Pallas kernels: none -> 32.5 us  [the longest x1 29.1 us: local(): pl.pallas_call(functools.partial(kernel, npair, nvirt, chunks), out_shape...]
    unnamed x1 -> x0, blocking collectives: 17.7 us -> none
    psum x1 -> x0, blocking collectives: 13.6 us -> none  [local(): couplings = lax.psum(partial_sums, 'virt')]
    dot_general x3 -> x0, matrix products: 4.26 us -> none  [the longest x1 3.8 us: local(): lax.dot_general(right_piece, flat_rdm, (((1,), (1,)), ((), ())), preferre...]
    gather x1 -> x0, local copies, waits for them, and re-layouts: 1.99 us -> none  [local(): jnp.take(lax.all_gather(vir_left, 'virt', axis=0, tiled=True), positions,...]
    unnamed x15 -> x2, local copies, waits for them, and re-layouts: 0.89 us -> 2.4 us
    add x3 -> x0, other arithmetic: 1.36 us -> none  [the longest x2 0.7 us: local(): row_block_starts[:, None] + virt_index * rows]
where the time goes in v1:
time: 37 us; the launch traced here: 36.8 us
  Pallas kernels  32.5 us (88%)
  local copies, waits for them, and re-layouts  3.67 us (10%)
  between operations  0.64 us (2%)
    pallas_call x1, Pallas kernels, local(): pl.pallas_call(functools.partial(kernel, npair, nvirt, chunks), out_shape...  29.1 us
    pallas_call x1, Pallas kernels, local(): pl.pallas_call(windows, out_shape=(jax.ShapeDtypeStruct((nvirt, avirt, wi...  3.32 us
    unnamed x2, local copies, waits for them, and re-layouts  2.4 us
    reshape x1, local copies, waits for them, and re-layouts, local(): bra_ket_states.T.reshape(2 * slots)  1.27 us

profile of v1, /device:TPU:0, one launch (start us, length us, event | category | flops | bytes accessed | tf_op | source)
XLA Modules:
  0.0 36.8 jit_solution(724427185402320845)
XLA Ops:
  0.6 1.3 %reshape.14.states_ref = s32[80]{0:T(128)} reshape(s32[2,40]{1,0:T(2,128)} %bitcast.4) | data formatting | bytes 640 | tf_op jit(solution)/shard_map/reshape | solution.py:363
  1.9 3.3 %shard_map.86 = (bf16[8,16,768]{2,1,0:T(8,128)(2,1)}, f32[1,640]{1,0:T(1,128)}, s32[1,128]{1,0:T(1,128)}, s32[1,128]{1,0:T(1,128)}) custom-call(bf16[16,2744]{1,0:T(8,128)(2,1)} %l_raw.1, bf16[1,16]{1,0:T(2,128)(2,1)} %bitcast.3, f32[8]{0:T(128)} %se_ref.3, s32[80]{0:T(128)} %reshape.14.states_ref, s32[40]{0:T(128)} %starts_ref.1), custom_call_target="tpu_custom_call" | custom-call | tf_op jit(solution)/shard_map/pallas_call | solution.py:348
  5.2 29.1 %shard_map.87 = (f32[1,40]{1,0:T(1,128)}, f32[8,8]{1,0:T(8,128)}) custom-call(bf16[40,16,2744]{2,1,0:T(8,128)(2,1)} %d_hbm.1, bf16[16,2744]{1,0:T(8,128)(2,1)} %r_hbm.1, bf16[8,16,768]{2,1,0:T(8,128)(2,1)} %get-tuple-element.8.w_send, f32[1,640]{1,0:T(1,128)} %get-tuple-element.9.shift_ref, s32[1,128]{1,0:T(1,128)} %get-tuple-element.10.bra_ref, ...), custom_call_target="tpu_custom_call" | custom-call | tf_op jit(solution)/shard_map/pallas_call | solution.py:366
  34.4 1.1 %copy.11 = f32[40]{0:T(128)} copy(f32[40]{0:T(128)} %bitcast.5) | data formatting | bytes 320
  35.5 1.3 %copy.12 = f32[8,8]{1,0:T(8,128)} copy(f32[8,8]{1,0:T(8,128)} %get-tuple-element.17) | data formatting | bytes 512

commit v2 on v1

v2 whole, which is shorter than its diff:
```python
import functools

import jax
import jax.numpy as jnp
from jax import lax
from jax.experimental import pallas as pl
from jax.experimental.pallas import tpu as pltpu
from jax.sharding import PartitionSpec as P

MESH = pl.DeviceIdType.MESH
LANES = 128


def windows(
    l_raw,
    r_raw,
    e_ref,
    se_ref,
    states_ref,
    starts_ref,
    w_send,
    r_own,
    shift_ref,
    place_ref,
    l_f32,
):
    nvirt, avirt, _ = w_send.shape
    ntrip = l_raw.shape[1]
    slots = starts_ref.shape[0]
    rows = shift_ref.shape[1] // slots
    group = LANES // rows
    blocks = slots // group

    l_f32[...] = jnp.zeros_like(l_f32)
    l_f32[:, :ntrip] = l_raw[...].astype(jnp.float32)
    lane = lax.broadcasted_iota(jnp.int32, (avirt, LANES), 1) // rows
    width = rows * nvirt
    load_width = width + LANES

    def window_block(b, carry):
        views = []
        for j in range(group):
            offset = starts_ref[b * group + j]
            rest = offset % LANES
            base = pl.multiple_of(offset - rest, LANES)
            wide = l_f32[:, pl.ds(base, load_width)]
            turned = pltpu.roll(wide, (load_width - rest) % load_width, 1)
            views.append(turned[:, :width])
        for q in range(nvirt // group):
            held = [v[:, q * LANES : (q + 1) * LANES] for v in views]
            bit = 1
            while bit < group:
                keep = (lane & bit) == 0
                fresh = list(held)
                for j in range(group):
                    if j & bit == 0:
                        a, o = held[j], held[j | bit]
                        fresh[j] = jnp.where(keep, a, pltpu.roll(o, bit * rows, 1))
                        fresh[j | bit] = jnp.where(keep, pltpu.roll(a, LANES - bit * rows, 1), o)
                held = fresh
                bit *= 2
            for i in range(group):
                w_send[q * group + i, :, pl.ds(pl.multiple_of(b * LANES, LANES), LANES)] = held[
                    i
                ].astype(jnp.bfloat16)
        return carry

    lax.fori_loop(0, blocks, window_block, 0)
    square = (
        lax.broadcasted_iota(jnp.int32, (avirt, avirt), 0)
        == lax.broadcasted_iota(jnp.int32, (avirt, avirt), 1)
    )
    energy_own = jnp.sum(
        jnp.where(square, e_ref[...].astype(jnp.float32), 0.0), axis=1, keepdims=True
    )
    half = r_own.shape[2]
    rest = ntrip - half
    r_own[0] = r_raw[:, :half]
    r_own[1] = jnp.concatenate(
        [r_raw[:, half:], jnp.broadcast_to(energy_own, (avirt, half - rest)).astype(jnp.bfloat16)],
        axis=1,
    )

    wide_lane = lax.broadcasted_iota(jnp.int32, (1, LANES), 1)
    lane_of = lax.broadcasted_iota(jnp.int32, (rows, LANES), 1)
    nstate = se_ref.shape[0]
    shifts = []
    for b in range(blocks):
        shift = jnp.zeros((1, LANES), jnp.float32)
        for j in range(group):
            s = b * group + j
            i_state, j_state = states_ref[0, s], states_ref[1, s]
            total = se_ref[i_state] + se_ref[j_state]
            shift = jnp.where(wide_lane // rows == j, total, shift)
            code = LANES // 2 + i_state * nstate + j_state
            place_ref[s * rows : (s + 1) * rows, :] = (
                ((lane_of == s) | (lane_of == code)).astype(jnp.float32).astype(jnp.bfloat16)
            )
        shifts.append(shift)
    shift_ref[...] = jnp.concatenate(shifts, axis=1)


def kernel(
    npair,
    nvirt,
    d_hbm,
    w_send,
    r_own,
    shift_ref,
    place_ref,
    out_ref,
    d_all,
    r_all,
    w_all,
    p_send,
    p_all,
    h_send,
    h_all,
    d_sem,
    o_sem,
    own_sem,
    z_ssem,
    b_ssem,
    x_ssem,
    f_ssem,
    r_rsem,
    w_ssem,
    w_rsem,
    p_ssem,
    p_rsem,
    h_ssem,
    h_rsem,
):
    slots, rows, ntrip = d_all.shape
    _, _, avirt, half = r_all.shape
    rest = ntrip - half
    nz = nvirt // 2
    me = lax.axis_index("virt")
    my_pair = lax.axis_index("pair")
    my_z, my_c = me // 2, me % 2
    sibling = my_z * 2 + 1 - my_c
    mine = my_pair % 2
    partner = my_pair + 1 - 2 * mine
    z_order = sorted(range(1, nz), key=lambda d: -min(d, nz - d))

    r_copies = [
        pltpu.make_async_copy(r_own.at[h], r_all.at[h, me], o_sem.at[h]) for h in range(2)
    ]
    for copy in r_copies:
        copy.start()
    d_copy = pltpu.make_async_copy(d_hbm, d_all, d_sem)
    d_copy.start()

    barrier = pltpu.get_barrier_semaphore()
    for k in range(1, nvirt):
        pl.semaphore_signal(
            barrier, inc=1, device_id={"virt": (me + k) % nvirt}, device_id_type=MESH
        )
    for k in range(1, npair):
        pl.semaphore_signal(
            barrier, inc=1, device_id={"pair": (my_pair + k) % npair}, device_id_type=MESH
        )
    pl.semaphore_wait(barrier, nvirt + npair - 2)

    def send_right(h, source, device, send_sem, own=False):
        return pltpu.make_async_remote_copy(
            src_ref=r_own.at[h] if own else r_all.at[h, source],
            dst_ref=r_all.at[h, source],
            send_sem=send_sem,
            recv_sem=r_rsem.at[h, source],
            device_id=device,
            device_id_type=MESH,
        )

    sends = []

    def go(copy):
        copy.start()
        sends.append(copy)

    def same_core(dz):
        return ((my_z + dz) % nz) * 2 + my_c

    for dz in z_order:
        go(send_right(mine, me, {"virt": same_core(dz)}, z_ssem.at[dz], True))
    for h in range(2):
        go(send_right(h, me, {"virt": sibling}, b_ssem.at[h], True))
    for k in [2 * dz + o for dz in z_order for o in (0, 1)] + [1]:
        target = (me + k) % nvirt
        go(
            pltpu.make_async_remote_copy(
                src_ref=w_send.at[target],
                dst_ref=w_all.at[me],
                send_sem=w_ssem.at[k],
                recv_sem=w_rsem.at[me],
                device_id={"virt": target},
                device_id_type=MESH,
            )
        )
    own = pltpu.make_async_copy(w_send.at[me], w_all.at[me], own_sem)
    own.start()

    z_near = z_order[::-1]
    for dz in z_near:
        source = same_core(dz)
        send_right(mine, source, {"virt": sibling}, f_ssem.at[0, dz]).wait_recv()
        go(send_right(mine, source, {"pair": partner}, x_ssem.at[dz]))
        go(send_right(mine, source, {"virt": sibling}, f_ssem.at[0, dz]))
    for dz in z_near:
        source = same_core(dz)
        send_right(1 - mine, source, {"virt": sibling}, f_ssem.at[1, dz]).wait_recv()
        go(send_right(1 - mine, source, {"virt": sibling}, f_ssem.at[1, dz]))
    d_copy.wait()
    for copy in r_copies:
        copy.wait()
    for dz in range(nz):
        source = ((my_z + dz) % nz) * 2 + 1 - my_c
        for h in range(2):
            send_right(h, source, {"virt": sibling}, f_ssem.at[0, 0]).wait_recv()
    total = None
    for h, (lo, cw) in enumerate(((0, half), (half, rest))):
        part = lax.dot_general(
            r_all[h, :, :, :cw].reshape(nvirt * avirt, cw),
            d_all[:, :, lo : lo + cw].reshape(slots * rows, cw),
            (((1,), (1,)), ((), ())),
            preferred_element_type=jnp.float32,
        )
        total = part if total is None else total + part
    energy = r_all[1, :, :, half - LANES :].reshape(nvirt * avirt, LANES)[:, LANES - 1 :]
    inverse = 1.0 / (energy.astype(jnp.float32) - shift_ref[...])
    total = total * inverse
    own.wait()
    for k in range(1, nvirt):
        source = (me + k) % nvirt
        pltpu.make_async_remote_copy(
            src_ref=w_send.at[source],
            dst_ref=w_all.at[source],
            send_sem=w_ssem.at[0],
            recv_sem=w_rsem.at[source],
            device_id={"virt": source},
            device_id_type=MESH,
        ).wait_recv()
    columns = w_all[...].reshape(nvirt * avirt, slots * rows)
    summed = jnp.sum(total * columns.astype(jnp.float32), axis=0, keepdims=True)
    high = summed.astype(jnp.bfloat16).astype(jnp.float32)
    middle = (summed - high).astype(jnp.bfloat16).astype(jnp.float32)
    low = summed - high - middle
    terms = jnp.concatenate(
        [high, middle, low, jnp.zeros((5, slots * rows), jnp.float32)], axis=0
    ).astype(jnp.bfloat16)
    placed = jnp.dot(terms, place_ref[...], preferred_element_type=jnp.float32)
    partial = jnp.sum(placed, axis=0, keepdims=True)

    p_send[...] = partial
    for k in list(range(1, nvirt))[::-1]:
        target = (me + k) % nvirt
        go(
            pltpu.make_async_remote_copy(
                src_ref=p_send,
                dst_ref=p_all.at[me],
                send_sem=p_ssem.at[k],
                recv_sem=p_rsem.at[me],
                device_id={"virt": target},
                device_id_type=MESH,
            )
        )
    p_all[me] = partial
    for k in range(1, nvirt):
        source = (me + k) % nvirt
        pltpu.make_async_remote_copy(
            src_ref=p_send,
            dst_ref=p_all.at[source],
            send_sem=p_ssem.at[0],
            recv_sem=p_rsem.at[source],
            device_id={"virt": source},
            device_id_type=MESH,
        ).wait_recv()
    along = jnp.sum(p_all[...], axis=0)
    h_send[...] = along
    for k in range(1, npair):
        target = (my_pair + k) % npair
        go(
            pltpu.make_async_remote_copy(
                src_ref=h_send,
                dst_ref=h_all.at[my_pair],
                send_sem=h_ssem.at[k],
                recv_sem=h_rsem.at[my_pair],
                device_id={"pair": target},
                device_id_type=MESH,
            )
        )
    h_all[my_pair] = along
    for k in range(1, npair):
        source = (my_pair + k) % npair
        pltpu.make_async_remote_copy(
            src_ref=h_send,
            dst_ref=h_all.at[source],
            send_sem=h_ssem.at[0],
            recv_sem=h_rsem.at[source],
            device_id={"pair": source},
            device_id_type=MESH,
        ).wait_recv()
    lane = lax.broadcasted_iota(jnp.int32, (1, LANES), 1)
    out_ref[...] = jnp.where(lane < LANES // 2, along, jnp.sum(h_all[...], axis=0))
    for send in sends:
        send.wait_send()


def finish(row_ref, se_ref, coup_ref, heff_ref):
    slots, nstate = coup_ref.shape[1], heff_ref.shape[0]
    row = row_ref[...]
    coup_ref[...] = row[:, :slots]
    line = lax.broadcasted_iota(jnp.int32, (nstate, LANES), 0)
    lane = lax.broadcasted_iota(jnp.int32, (nstate, LANES), 1) - LANES // 2
    si = lax.broadcasted_iota(jnp.int32, (nstate, nstate), 0)
    sj = lax.broadcasted_iota(jnp.int32, (nstate, nstate), 1)
    heff = jnp.zeros((nstate, nstate), jnp.float32)
    for n in range(nstate):
        down = jnp.sum(jnp.where(lane == line * nstate + n, row, 0.0), axis=1, keepdims=True)
        up = jnp.sum(jnp.where(lane == n * nstate + line, row, 0.0), axis=1, keepdims=True)
        column = 0.5 * (down + up)
        heff = jnp.where(sj == n, column + jnp.where(si == n, se_ref[n], 0.0), heff)
    heff_ref[...] = heff


def local(
    npair,
    nvirt,
    density_row_blocks,
    vir_left,
    vir_right,
    orb_energy,
    state_energy,
    bra_ket_states,
    row_block_starts,
):
    slots, rows, ntrip = density_row_blocks.shape
    avirt = vir_left.shape[0]
    nstate = state_energy.shape[0]
    padded = -(-ntrip // LANES) * LANES
    half = -(-(ntrip + 1) // (2 * LANES)) * LANES
    hbm = pl.BlockSpec(memory_space=pltpu.HBM)
    vmem = pl.BlockSpec(memory_space=pltpu.VMEM)
    smem = pl.BlockSpec(memory_space=pltpu.SMEM)
    dma = pltpu.SemaphoreType.DMA
    nz = nvirt // 2
    cut = pl.pallas_call(
        windows,
        out_shape=(
            jax.ShapeDtypeStruct((nvirt, avirt, slots * rows), jnp.bfloat16),
            jax.ShapeDtypeStruct((2, avirt, half), jnp.bfloat16),
            jax.ShapeDtypeStruct((1, slots * rows), jnp.float32),
            jax.ShapeDtypeStruct((slots * rows, LANES), jnp.bfloat16),
        ),
        in_specs=[vmem, vmem, vmem, smem, smem, smem],
        out_specs=(vmem,) * 4,
        scratch_shapes=[pltpu.VMEM((avirt, padded + nvirt * rows), jnp.float32)],
    )(
        vir_left,
        vir_right,
        orb_energy.reshape(1, avirt),
        state_energy,
        bra_ket_states.T,
        row_block_starts,
    )
    row = pl.pallas_call(
        functools.partial(kernel, npair, nvirt),
        out_shape=jax.ShapeDtypeStruct((1, LANES), jnp.float32),
        in_specs=[hbm, vmem, vmem, vmem, vmem],
        out_specs=vmem,
        scratch_shapes=[
            pltpu.VMEM((slots, rows, ntrip), jnp.bfloat16),
            pltpu.VMEM((2, nvirt, avirt, half), jnp.bfloat16),
            pltpu.VMEM((nvirt, avirt, slots * rows), jnp.bfloat16),
            pltpu.VMEM((1, LANES), jnp.float32),
            pltpu.VMEM((nvirt, 1, LANES), jnp.float32),
            pltpu.VMEM((1, LANES), jnp.float32),
            pltpu.VMEM((npair, 1, LANES), jnp.float32),
            dma,
            dma((2,)),
            dma,
            dma((nz,)),
            dma((2,)),
            dma((nz,)),
            dma((2, nz)),
            dma((2, nvirt)),
            dma((nvirt,)),
            dma((nvirt,)),
            dma((nvirt,)),
            dma((nvirt,)),
            dma((npair,)),
            dma((npair,)),
        ],
        compiler_params=pltpu.CompilerParams(
            collective_id=0, has_side_effects=True, vmem_limit_bytes=60 * 1024 * 1024
        ),
    )(density_row_blocks, *cut)
    couplings, heff = pl.pallas_call(
        finish,
        out_shape=(
            jax.ShapeDtypeStruct((1, slots), jnp.float32),
            jax.ShapeDtypeStruct((nstate, nstate), jnp.float32),
        ),
        in_specs=[vmem, smem],
        out_specs=(vmem, vmem),
    )(row, state_energy)
    return couplings.reshape(slots), heff


def solution(mesh):
    npair, nvirt = mesh.shape["pair"], mesh.shape["virt"]
    placed = (
        P("pair", "virt", None),
        P("virt", None),
        P("virt", None),
        P("virt"),
        P(),
        P("pair", None),
        P("pair"),
    )
    return jax.shard_map(
        functools.partial(local, npair, nvirt),
        mesh=mesh,
        in_specs=placed,
        out_specs=(P("pair"), P()),
        check_vma=False,
    )
```

time: 37 us -> 33.2 us (0.90)
  local copies, waits for them, and re-layouts: 3.67 us -> 0 us
    unnamed x2 -> x0, local copies, waits for them, and re-layouts: 2.4 us -> none
    reshape x1 -> x0, local copies, waits for them, and re-layouts: 1.27 us -> none  [local(): bra_ket_states.T.reshape(2 * slots)]
    pallas_call x2 -> x3, Pallas kernels: 32.5 us -> 32.3 us  [the longest x1 27.4 us: local(): pl.pallas_call(functools.partial(kernel, npair, nvirt), out_shape=jax.Sha...]
where the time goes in v2:
time: 33.2 us; the launch traced here: 33 us
  Pallas kernels  32.3 us (97%)
  between operations  0.64 us (2%)
    pallas_call x1, Pallas kernels, local(): pl.pallas_call(functools.partial(kernel, npair, nvirt), out_shape=jax.Sha...  27.4 us
    pallas_call x1, Pallas kernels, local(): pl.pallas_call(windows, out_shape=(jax.ShapeDtypeStruct((nvirt, avirt, sl...  3.44 us
    pallas_call x1, Pallas kernels, local(): pl.pallas_call(finish, out_shape=(jax.ShapeDtypeStruct((1, slots), jnp.fl...  1.49 us

profile of v2, /device:TPU:0, one launch (start us, length us, event | category | flops | bytes accessed | tf_op | source)
XLA Modules:
  0.0 33.0 jit_solution(11813115092518553486)
XLA Ops:
  0.6 3.4 %shard_map.86 = (bf16[8,16,640]{2,1,0:T(8,128)(2,1)}, bf16[2,16,1408]{2,1,0:T(8,128)(2,1)}, f32[1,640]{1,0:T(1,128)}, bf16[640,128]{1,0:T(8,128)(2,1)}) custom-call(bf16[16,2744]{1,0:T(8,128)(2,1)} %l_raw.1, bf16[16,2744]{1,0:T(8,128)(2,1)} %r_raw.1, bf16[1,16]{1,0:T(2,128)(2,1)} %bitcast.4, f32[8]{0:T(128)} %se_ref.3, s32[2,40]{1,0:T(2,128)} %bitcast.3, ...), custom_call_target="tpu_custom_call" | custom-call | tf_op jit(solution)/shard_map/pallas_call | solution.py:347
  4.1 27.4 %shard_map.87.row_ref = f32[1,128]{1,0:T(1,128)} custom-call(bf16[40,16,2744]{2,1,0:T(8,128)(2,1)} %d_hbm.1, bf16[8,16,640]{2,1,0:T(8,128)(2,1)} %get-tuple-element.8.w_send, bf16[2,16,1408]{2,1,0:T(8,128)(2,1)} %get-tuple-element.9.r_own, f32[1,640]{1,0:T(1,128)} %get-tuple-element.10.shift_ref, bf16[640,128]{1,0:T(8,128)(2,1)} %get-tuple-element.11.place_ref), custom_call_target="tpu_custom_call" | custom-call | tf_op jit(solution)/shard_map/pallas_call | solution.py:366
  31.5 1.5 %shard_map.88 = (f32[1,40]{1,0:T(1,128)}, f32[8,8]{1,0:T(8,128)}) custom-call(f32[1,128]{1,0:T(1,128)} %shard_map.87.row_ref, f32[8]{0:T(128)} %se_ref.3), custom_call_target="tpu_custom_call" | custom-call | tf_op jit(solution)/shard_map/pallas_call | solution.py:398

commit v3 on v2

--- a/solution.py
+++ b/solution.py
@@ -114,8 +114,6 @@
     w_all,
     p_send,
     p_all,
-    h_send,
-    h_all,
     d_sem,
     o_sem,
     own_sem,
@@ -128,8 +126,7 @@
     w_rsem,
     p_ssem,
     p_rsem,
-    h_ssem,
-    h_rsem,
+    far_sem,
 ):
     slots, rows, ntrip = d_all.shape
     _, _, avirt, half = r_all.shape
@@ -161,6 +158,10 @@
             barrier, inc=1, device_id={"pair": (my_pair + k) % npair}, device_id_type=MESH
         )
     pl.semaphore_wait(barrier, nvirt + npair - 2)
+    for k in range(1, npair):
+        pl.semaphore_signal(
+            far_sem, inc=1, device_id={"pair": (my_pair + k) % npair}, device_id_type=MESH
+        )
 
     def send_right(h, source, device, send_sem, own=False):
         return pltpu.make_async_remote_copy(
@@ -251,57 +252,41 @@
     placed = jnp.dot(terms, place_ref[...], preferred_element_type=jnp.float32)
     partial = jnp.sum(placed, axis=0, keepdims=True)
 
+    pl.semaphore_wait(far_sem, npair - 1)
+    count = npair * nvirt
+    number = my_pair * nvirt + me
     p_send[...] = partial
-    for k in list(range(1, nvirt))[::-1]:
-        target = (me + k) % nvirt
-        go(
-            pltpu.make_async_remote_copy(
-                src_ref=p_send,
-                dst_ref=p_all.at[me],
-                send_sem=p_ssem.at[k],
-                recv_sem=p_rsem.at[me],
-                device_id={"virt": target},
-                device_id_type=MESH,
-            )
-        )
-    p_all[me] = partial
-    for k in range(1, nvirt):
-        source = (me + k) % nvirt
-        pltpu.make_async_remote_copy(
+
+    def row_copy(k, own):
+        other = lax.rem(number + k, count)
+        return pltpu.make_async_remote_copy(
             src_ref=p_send,
-            dst_ref=p_all.at[source],
-            send_sem=p_ssem.at[0],
-            recv_sem=p_rsem.at[source],
-            device_id={"virt": source},
+            dst_ref=p_all.at[number if own else other],
+            send_sem=p_ssem.at[k],
+            recv_sem=p_rsem.at[number if own else other],
+            device_id={"pair": lax.div(other, nvirt), "virt": lax.rem(other, nvirt)},
             device_id_type=MESH,
-        ).wait_recv()
-    along = jnp.sum(p_all[...], axis=0)
-    h_send[...] = along
-    for k in range(1, npair):
-        target = (my_pair + k) % npair
-        go(
-            pltpu.make_async_remote_copy(
-                src_ref=h_send,
-                dst_ref=h_all.at[my_pair],
-                send_sem=h_ssem.at[k],
-                recv_sem=h_rsem.at[my_pair],
-                device_id={"pair": target},
-                device_id_type=MESH,
-            )
-        )
-    h_all[my_pair] = along
-    for k in range(1, npair):
-        source = (my_pair + k) % npair
-        pltpu.make_async_remote_copy(
-            src_ref=h_send,
-            dst_ref=h_all.at[source],
-            send_sem=h_ssem.at[0],
-            recv_sem=h_rsem.at[source],
-            device_id={"pair": source},
-            device_id_type=MESH,
-        ).wait_recv()
+        )
+
+    def send_row(k, carry):
+        row_copy(k, True).start()
+        return carry
+
+    def take_row(k, carry):
+        row_copy(k, False).wait_recv()
+        return carry
+
+    def end_row(k, carry):
+        row_copy(k, True).wait_send()
+        return carry
+
+    lax.fori_loop(1, count, send_row, 0, unroll=count <= 64)
+    p_all[number] = partial
+    lax.fori_loop(1, count, take_row, 0, unroll=count <= 64)
+    along = jnp.sum(p_all[pl.ds(my_pair * nvirt, nvirt)], axis=0)
     lane = lax.broadcasted_iota(jnp.int32, (1, LANES), 1)
-    out_ref[...] = jnp.where(lane < LANES // 2, along, jnp.sum(h_all[...], axis=0))
+    out_ref[...] = jnp.where(lane < LANES // 2, along, jnp.sum(p_all[...], axis=0))
+    lax.fori_loop(1, count, end_row, 0, unroll=count <= 64)
     for send in sends:
         send.wait_send()
 
@@ -373,9 +358,7 @@
             pltpu.VMEM((2, nvirt, avirt, half), jnp.bfloat16),
             pltpu.VMEM((nvirt, avirt, slots * rows), jnp.bfloat16),
             pltpu.VMEM((1, LANES), jnp.float32),
-            pltpu.VMEM((nvirt, 1, LANES), jnp.float32),
-            pltpu.VMEM((1, LANES), jnp.float32),
-            pltpu.VMEM((npair, 1, LANES), jnp.float32),
+            pltpu.VMEM((npair * nvirt, 1, LANES), jnp.float32),
             dma,
             dma((2,)),
             dma,
@@ -386,10 +369,9 @@
             dma((2, nvirt)),
             dma((nvirt,)),
             dma((nvirt,)),
-            dma((nvirt,)),
-            dma((nvirt,)),
-            dma((npair,)),
-            dma((npair,)),
+            dma((npair * nvirt,)),
+            dma((npair * nvirt,)),
+            pltpu.SemaphoreType.REGULAR,
         ],
         compiler_params=pltpu.CompilerParams(
             collective_id=0, has_side_effects=True, vmem_limit_bytes=60 * 1024 * 1024

time: 33.2 us -> 31.5 us (0.949)
  Pallas kernels: 32.3 us -> 30.7 us
    pallas_call x1, Pallas kernels: 27.4 us -> 25.8 us  [local(): pl.pallas_call(functools.partial(kernel, npair, nvirt), out_shape=jax.Sha...]
where the time goes in v3:
time: 31.5 us; the launch traced here: 31.4 us
  Pallas kernels  30.7 us (97%)
  between operations  0.64 us (2%)
    pallas_call x1, Pallas kernels, local(): pl.pallas_call(functools.partial(kernel, npair, nvirt), out_shape=jax.Sha...  25.8 us
    pallas_call x1, Pallas kernels, local(): pl.pallas_call(windows, out_shape=(jax.ShapeDtypeStruct((nvirt, avirt, sl...  3.44 us
    pallas_call x1, Pallas kernels, local(): pl.pallas_call(finish, out_shape=(jax.ShapeDtypeStruct((1, slots), jnp.fl...  1.49 us

profile of v3, /device:TPU:0, one launch (start us, length us, event | category | flops | bytes accessed | tf_op | source)
XLA Modules:
  0.0 31.4 jit_solution(12779481025472194995)
XLA Ops:
  0.6 3.4 %shard_map.86 = (bf16[8,16,640]{2,1,0:T(8,128)(2,1)}, bf16[2,16,1408]{2,1,0:T(8,128)(2,1)}, f32[1,640]{1,0:T(1,128)}, bf16[640,128]{1,0:T(8,128)(2,1)}) custom-call(bf16[16,2744]{1,0:T(8,128)(2,1)} %l_raw.1, bf16[16,2744]{1,0:T(8,128)(2,1)} %r_raw.1, bf16[1,16]{1,0:T(2,128)(2,1)} %bitcast.4, f32[8]{0:T(128)} %se_ref.3, s32[2,40]{1,0:T(2,128)} %bitcast.3, ...), custom_call_target="tpu_custom_call" | custom-call | tf_op jit(solution)/shard_map/pallas_call | solution.py:332
  4.1 25.8 %shard_map.87.row_ref = f32[1,128]{1,0:T(1,128)} custom-call(bf16[40,16,2744]{2,1,0:T(8,128)(2,1)} %d_hbm.1, bf16[8,16,640]{2,1,0:T(8,128)(2,1)} %get-tuple-element.8.w_send, bf16[2,16,1408]{2,1,0:T(8,128)(2,1)} %get-tuple-element.9.r_own, f32[1,640]{1,0:T(1,128)} %get-tuple-element.10.shift_ref, bf16[640,128]{1,0:T(8,128)(2,1)} %get-tuple-element.11.place_ref), custom_call_target="tpu_custom_call" | custom-call | tf_op jit(solution)/shard_map/pallas_call | solution.py:351
  29.9 1.5 %shard_map.88 = (f32[1,40]{1,0:T(1,128)}, f32[8,8]{1,0:T(8,128)}) custom-call(f32[1,128]{1,0:T(1,128)} %shard_map.87.row_ref, f32[8]{0:T(128)} %se_ref.3), custom_call_target="tpu_custom_call" | custom-call | tf_op jit(solution)/shard_map/pallas_call | solution.py:380
